TPU v7x, 32 devices: a whole 2x2x4 slice. The times are simulated.
32 devices in a mesh: sx: 8 (over z, y), sy: 4 (over x, core).
Axes of the slice: x: 2, y: 2, z: 4, core: 2. Of those that a mesh axis runs over, the one named last changes fastest.
Arguments:
- tensors: bfloat16 [2, 8, 4, 1024, 256], P(None, 'sx', 'sy'), may hold values from -6 to 6
- gates: bfloat16 [5, 2, 2, 256, 256], replicated, may hold values from -0.1875 to 0.1875
- closing_rows: bfloat16 [2, 4096, 1024], P(None, ('sx', 'sy')), may hold values from -0.125 to 0.125
- closing_columns: float32 [2, 4096, 256], P(None, ('sx', 'sy')), may hold values from -0.25 to 0.25
Outputs:
- amplitudes: float32 [2, 4096], replicated
All inputs are finite; a program needn't handle non-finite values.
Results may differ from a plain program's by a relative error of at most 0.012.
Values may be sent and summed in bfloat16 or wider, within the bound.
A program may use at most 64 MiB of HBM per device.

v0:
```python
import jax
import jax.numpy as jnp
from jax import lax
from jax.sharding import PartitionSpec as P


def mixing_matrix(gate_pair, sign):
    own_top = jnp.concatenate([gate_pair[0, 0], gate_pair[0, 1]], axis=1)
    own_low = jnp.concatenate([-gate_pair[0, 1], gate_pair[0, 0]], axis=1)
    far_top = jnp.concatenate([gate_pair[1, 0], gate_pair[1, 1]], axis=1) * sign
    far_low = jnp.concatenate([-gate_pair[1, 1], gate_pair[1, 0]], axis=1) * sign
    return jnp.concatenate([own_top, own_low, far_top, far_low], axis=0)


def combine(own, partner, matrix):
    width = own.shape[-1]
    leading = own.shape[1:-1]
    joined = jnp.concatenate([own[0], own[1], partner[0], partner[1]], axis=-1).reshape(
        -1, 4 * width
    )
    result = jnp.dot(joined, matrix, preferred_element_type=jnp.float32).astype(jnp.bfloat16)
    real_part = result[:, :width].reshape(leading + (width,))
    imag_part = result[:, width:].reshape(leading + (width,))
    return jnp.stack([real_part, imag_part])


def local_section(grouped, gate_pair, axis_dim, bit_pos):
    shape = grouped.shape
    count = shape[axis_dim]
    split = shape[:axis_dim] + (count >> bit_pos + 1, 2, 1 << bit_pos) + shape[axis_dim + 1 :]
    blocks = grouped.reshape(split)
    lower = lax.index_in_dim(blocks, 0, axis_dim + 1, keepdims=False)
    upper = lax.index_in_dim(blocks, 1, axis_dim + 1, keepdims=False)
    new_lower = combine(lower, upper, mixing_matrix(gate_pair, 1.0))
    new_upper = combine(upper, lower, mixing_matrix(gate_pair, -1.0))
    return jnp.stack([new_lower, new_upper], axis=axis_dim + 1).reshape(shape)


def close_columns(projected, closing_columns):
    amp_real = jnp.sum(
        projected[0] * closing_columns[0] - projected[1] * closing_columns[1], axis=-1
    )
    amp_imag = jnp.sum(
        projected[0] * closing_columns[1] + projected[1] * closing_columns[0], axis=-1
    )
    return jnp.stack([amp_real, amp_imag])


def combine_rows(closing_rows, current):
    proj_real = jnp.dot(closing_rows[0], current[0], preferred_element_type=jnp.float32) - jnp.dot(
        closing_rows[1], current[1], preferred_element_type=jnp.float32
    )
    proj_imag = jnp.dot(closing_rows[0], current[1], preferred_element_type=jnp.float32) + jnp.dot(
        closing_rows[1], current[0], preferred_element_type=jnp.float32
    )
    return jnp.stack([proj_real, proj_imag])


def local(tensors, gates, closing_rows, closing_columns):
    current = tensors[:, 0, 0]
    rows_dev = current.shape[1]
    width = current.shape[2]
    count_x = lax.axis_size("sx")
    count_y = lax.axis_size("sy")
    bits_x = count_x.bit_length() - 1
    bits_y = count_y.bit_length() - 1
    grouped = lax.all_to_all(
        current.reshape(2, count_x, rows_dev // count_x, width),
        "sx",
        split_axis=1,
        concat_axis=1,
        tiled=True,
    )
    for bit_pos in range(bits_x):
        grouped = local_section(grouped, gates[bit_pos], 1, bit_pos)
    current = lax.all_to_all(grouped, "sx", split_axis=1, concat_axis=1, tiled=True).reshape(
        2, rows_dev, width
    )
    grouped = lax.all_to_all(
        current.reshape(2, count_y, rows_dev // count_y, width),
        "sy",
        split_axis=1,
        concat_axis=1,
        tiled=True,
    )
    for bit_pos in range(bits_y):
        grouped = local_section(grouped, gates[bits_x + bit_pos], 1, bit_pos)
    current = lax.all_to_all(grouped, "sy", split_axis=1, concat_axis=1, tiled=True).reshape(
        2, rows_dev, width
    )
    closed = close_columns(combine_rows(closing_rows, current), closing_columns)
    return lax.all_gather(closed, ("sx", "sy"), axis=1, tiled=True)


def solution(mesh):
    placed = (
        P(None, "sx", "sy", None, None),
        P(),
        P(None, ("sx", "sy"), None),
        P(None, ("sx", "sy"), None),
    )
    return jax.shard_map(local, mesh=mesh, in_specs=placed, out_specs=P(), check_vma=False)
```

profile of v0, /device:TPU:0, one launch (start us, length us, event | category | flops | bytes accessed | tf_op | source)
XLA Modules:
  0.0 157.4 jit_solution(10815839486201930402)
XLA Ops:
  0.0 2.3 %copy.47 = bf16[2,8,128,256]{3,2,0,1:T(8,128)(2,1)} copy(bf16[2,8,128,256]{3,2,1,0:T(8,128)(2,1)} %bitcast.207) | data formatting | bytes 2097152 | tf_op jit(solution)/shard_map/reshape;squeeze | solution.py:68
  2.3 7.3 %all-to-all-start = ((bf16[2,8,128,256]{3,2,0,1:T(8,128)(2,1)}), bf16[2,8,128,256]{3,2,0,1:T(8,128)(2,1)S(1)}, u32[]{:S(2)}, u32[]{:S(2)}) async-start(bf16[2,8,128,256]{3,2,0,1:T(8,128)(2,1)} %copy.47), calls=%async_computation | async-start | bytes 2097152 | tf_op jit(solution)/shard_map/all_to_all | solution.py:67
  9.6 1.9 %slice_bitcast_fusion = (bf16[2,2,256,256]{3,2,1,0:T(8,128)(2,1)S(1)}, bf16[2,2,256,256]{3,2,1,0:T(8,128)(2,1)S(1)}, bf16[2,2,256,256]{3,2,1,0:T(8,128)(2,1)S(1)...) fusion(bf16[5,2,2,256,256]{4,3,2,1,0:T(8,128)(2,1)} %param.5), kind=kLoop, calls=%fused_computation.162 | loop fusion | bytes 5242880 | tf_op jit(solution)/shard_map/squeeze | solution.py:87
  11.5 0.7 slice_bitcast_fusion.23
  12.2 0.7 fusion.156
  13.0 0.9 maximum_multiply_fusion
  13.9 0.8 slice_bitcast_fusion.15
  14.7 0.9 maximum_multiply_fusion.2
  15.6 0.8 fusion.160
  16.3 0.9 maximum_multiply_fusion.4
  17.2 18.2 %all-to-all-done = bf16[2,8,128,256]{3,2,0,1:T(8,128)(2,1)S(1)} async-done(((bf16[2,8,128,256]{3,2,0,1:T(8,128)(2,1)}), bf16[2,8,128,256]{3,2,0,1:T(8,128)(2,1)S(1)}, u32[]{:S(2)}, u32[]{:S(2)}) %all-to-all-start) | async-done | bytes 1048608 | tf_op jit(solution)/shard_map/all_to_all | solution.py:67
  35.5 0.8 copy-done.23
  36.4 0.7 convolution_convert_fusion.9
  37.5 0.7 convolution_convert_fusion.8
  39.4 0.7 convolution_convert_fusion.7
  40.4 0.7 convolution_convert_fusion.6
  42.3 0.7 convolution_convert_fusion.5
  43.4 0.7 convolution_convert_fusion.4
  44.5 29.3 %all_to_all.20 = bf16[2,8,128,256]{3,2,0,1:T(8,128)(2,1)S(1)} all-to-all(bf16[2,8,128,256]{3,2,0,1:T(8,128)(2,1)S(1)} %copy.56), channel_id=1, replica_groups=mesh['sx'=8,'sy'=4] {'sx'}, dimensions={1} | all-to-all | bytes 2097152 | tf_op jit(solution)/shard_map/all_to_all | solution.py:76
  73.9 1.1 copy.58
  75.0 3.5 %all-to-all-start.2 = ((bf16[2,4,256,256]{3,2,0,1:T(8,128)(2,1)}), bf16[2,4,256,256]{3,2,0,1:T(8,128)(2,1)S(1)}, u32[]{:S(2)}, u32[]{:S(2)}) async-start(bf16[2,4,256,256]{3,2,0,1:T(8,128)(2,1)} %copy.58), calls=%async_computation.2 | async-start | bytes 2097152 | tf_op jit(solution)/shard_map/all_to_all | solution.py:79
  78.5 0.8 slice_bitcast_fusion.7
  79.3 0.9 maximum_multiply_fusion.6
  80.9 12.0 %all-to-all-done.2 = bf16[2,4,256,256]{3,2,0,1:T(8,128)(2,1)S(1)} async-done(((bf16[2,4,256,256]{3,2,0,1:T(8,128)(2,1)}), bf16[2,4,256,256]{3,2,0,1:T(8,128)(2,1)S(1)}, u32[]{:S(2)}, u32[]{:S(2)}) %all-to-all-start.2) | async-done | bytes 1048608 | tf_op jit(solution)/shard_map/all_to_all | solution.py:79
  93.0 0.7 convolution_convert_fusion.3
  94.1 0.7 convolution_convert_fusion.2
  96.0 0.7 convolution_convert_fusion.1
  96.7 0.7 convolution_convert_fusion
  97.8 1.1 copy.65
  98.9 3.5 %all-to-all-start.3 = ((bf16[2,4,256,256]{3,2,0,1:T(8,128)(2,1)}), bf16[2,4,256,256]{3,2,0,1:T(8,128)(2,1)S(1)}, u32[]{:S(2)}, u32[]{:S(2)}) async-start(bf16[2,4,256,256]{3,2,0,1:T(8,128)(2,1)} %copy.65), calls=%async_computation.3 | async-start | bytes 2097152 | tf_op jit(solution)/shard_map/all_to_all | solution.py:88
  102.6 14.2 %all-to-all-done.3 = bf16[2,4,256,256]{3,2,0,1:T(8,128)(2,1)S(1)} async-done(((bf16[2,4,256,256]{3,2,0,1:T(8,128)(2,1)}), bf16[2,4,256,256]{3,2,0,1:T(8,128)(2,1)S(1)}, u32[]{:S(2)}, u32[]{:S(2)}) %all-to-all-start.3) | async-done | bytes 1048608 | tf_op jit(solution)/shard_map/all_to_all | solution.py:88
  118.3 38.6 %all_gather.3 = f32[2,4096]{1,0:T(2,128)S(1)} all-gather(f32[2,128]{1,0:T(2,128)S(1)} %pad_maximum_fusion.3), channel_id=1, replica_groups=mesh['sx'=8,'sy'=4] {'sx','sy'}, dimensions={1}, use_global_device_ids=true | all-gather | bytes 33792 | tf_op jit(solution)/shard_map/all_gather | solution.py:92
  (97 shorter events, 8.7 us)
Async XLA Ops:
  2.3 33.1 %all-to-all-start = ((bf16[2,8,128,256]{3,2,0,1:T(8,128)(2,1)}), bf16[2,8,128,256]{3,2,0,1:T(8,128)(2,1)S(1)}, u32[]{:S(2)}, u32[]{:S(2)}) async-start(bf16[2,8,128,256]{3,2,0,1:T(8,128)(2,1)} %copy.47), calls=%async_computation | async-start | bytes 2097152 | tf_op jit(solution)/shard_map/all_to_all | solution.py:67
  35.4 0.9 copy-start.23
  35.4 1.0 copy-start.24
  35.4 1.0 copy-start.25
  36.4 0.9 copy-start.5
  36.4 1.0 copy-start.6
  38.4 0.9 copy-start.11
  38.4 1.0 copy-start.12
  38.4 1.0 copy-start.22
  39.4 0.9 copy-start.3
  39.4 1.0 copy-start.4
  41.4 0.9 copy-start.10
  41.4 1.0 copy-start.21
  42.3 0.9 copy-start.1
  42.3 1.0 copy-start.2
  75.0 17.9 %all-to-all-start.2 = ((bf16[2,4,256,256]{3,2,0,1:T(8,128)(2,1)}), bf16[2,4,256,256]{3,2,0,1:T(8,128)(2,1)S(1)}, u32[]{:S(2)}, u32[]{:S(2)}) async-start(bf16[2,4,256,256]{3,2,0,1:T(8,128)(2,1)} %copy.58), calls=%async_computation.2 | async-start | bytes 2097152 | tf_op jit(solution)/shard_map/all_to_all | solution.py:79
  79.2 13.7 %copy-start.14 = (bf16[256,256]{1,0:T(8,128)(2,1)S(1)}, bf16[256,256]{1,0:T(8,128)(2,1)}, u32[]{:S(2)}) copy-start(bf16[256,256]{1,0:T(8,128)(2,1)} %get-tuple-element.96) | copy-start | bytes 393220
  79.2 13.7 %copy-start.16 = (bf16[256,256]{1,0:T(8,128)(2,1)S(1)}, bf16[256,256]{1,0:T(8,128)(2,1)}, u32[]{:S(2)}) copy-start(bf16[256,256]{1,0:T(8,128)(2,1)} %get-tuple-element.99) | copy-start | bytes 393220
  79.2 13.7 %copy-start.19 = (bf16[256,256]{1,0:T(8,128)(2,1)S(1)}, bf16[256,256]{1,0:T(8,128)(2,1)}, u32[]{:S(2)}) copy-start(bf16[256,256]{1,0:T(8,128)(2,1)} %get-tuple-element.107) | copy-start | bytes 393220
  93.0 1.0 copy-start.7
  93.0 1.0 copy-start.8
  93.0 1.0 copy-start.15
  93.0 1.1 copy-start.17
  93.0 1.1 copy-start.20
  95.0 0.9 copy-start.13
  95.1 1.0 copy-start.18
  97.8 4.6 %copy-start.9 = (f32[2,128,256]{2,1,0:T(8,128)S(1)}, f32[2,128,256]{2,1,0:T(8,128)}, u32[]{:S(2)}) copy-start(f32[2,128,256]{2,1,0:T(8,128)} %param.7) | copy-start | bytes 786436
  98.9 17.9 %all-to-all-start.3 = ((bf16[2,4,256,256]{3,2,0,1:T(8,128)(2,1)}), bf16[2,4,256,256]{3,2,0,1:T(8,128)(2,1)S(1)}, u32[]{:S(2)}, u32[]{:S(2)}) async-start(bf16[2,4,256,256]{3,2,0,1:T(8,128)(2,1)} %copy.65), calls=%async_computation.3 | async-start | bytes 2097152 | tf_op jit(solution)/shard_map/all_to_all | solution.py:88
  102.4 14.5 %copy-start = (bf16[2,128,1024]{2,1,0:T(8,128)(2,1)S(1)}, bf16[2,128,1024]{2,1,0:T(8,128)(2,1)}, u32[]{:S(2)}) copy-start(bf16[2,128,1024]{2,1,0:T(8,128)(2,1)} %param.6) | copy-start | bytes 1572868
where the time goes:
time: 158 us; the launch traced here: 157 us
  blocking collectives  67.9 us (43%)
  waiting for transfers between devices  44.3 us (28%)
  local copies, waits for them, and re-layouts  15.1 us (10%)
  starting transfers between devices  14.3 us (9%)
  matrix products  8.46 us (5%)
  other arithmetic  6.72 us (4%)
    all_gather x1, blocking collectives, local(): return lax.all_gather(closed, ('sx', 'sy'), axis=1, tiled=True)  38.6 us
    all_to_all x1, blocking collectives, local(): lax.all_to_all(grouped, 'sx', split_axis=1, concat_axis=1, tiled=True)  29.3 us
    all_to_all x1, waiting for transfers between devices, local(): lax.all_to_all(current.reshape(2, count_x, rows_dev // count_x, width), '...  18.2 us
    all_to_all x1, waiting for transfers between devices, local(): lax.all_to_all(grouped, 'sy', split_axis=1, concat_axis=1, tiled=True)  14.2 us
    all_to_all x1, waiting for transfers between devices, local(): lax.all_to_all(current.reshape(2, count_y, rows_dev // count_y, width), '...  12 us
    all_to_all x1, starting transfers between devices, local(): lax.all_to_all(current.reshape(2, count_x, rows_dev // count_x, width), '...  7.31 us
    dot_general x10, matrix products, combine(): jnp.dot(joined, matrix, preferred_element_type=jnp.float32)  7.1 us
    unnamed x59, local copies, waits for them, and re-layouts  5.51 us
  transfers between devices with their start and end apart: 3, of which 3 were waited for; matrix products, arithmetic and copies ran while one was open for 6% of the time, Pallas kernels for 0%

commit v1 on v0

--- a/solution.py
+++ b/solution.py
@@ -1,7 +1,16 @@
+import functools
 import jax
 import jax.numpy as jnp
 from jax import lax
 from jax.sharding import PartitionSpec as P
+
+
+def replace_the_inputs(z, axis_tag):
+    y = lax.all_gather(z, axis_tag)
+    return jnp.concatenate(y, axis=1)
+
+
+open_tables_over_axis = functools.partial(replace_the_inputs, axis_tag=("sx", "sy"))
 
 
 def mixing_matrix(gate_pair, sign):
@@ -89,7 +98,7 @@
         2, rows_dev, width
     )
     closed = close_columns(combine_rows(closing_rows, current), closing_columns)
-    return lax.all_gather(closed, ("sx", "sy"), axis=1, tiled=True)
+    return open_tables_over_axis(closed)
 
 
 def solution(mesh):

time: 158 us -> 158 us (level)
  no operation moved by 1% of the time
where the time goes in v1:
time: 158 us; the launch traced here: 157 us
  blocking collectives  67.9 us (43%)
  waiting for transfers between devices  44.3 us (28%)
  local copies, waits for them, and re-layouts  15.1 us (10%)
  starting transfers between devices  14.3 us (9%)
  matrix products  8.46 us (5%)
  other arithmetic  6.72 us (4%)
    all_gather x1, blocking collectives, replace_the_inputs(): y = lax.all_gather(z, axis_tag)  38.6 us
    all_to_all x1, blocking collectives, local(): lax.all_to_all(grouped, 'sx', split_axis=1, concat_axis=1, tiled=True)  29.3 us
    all_to_all x1, waiting for transfers between devices, local(): lax.all_to_all(current.reshape(2, count_x, rows_dev // count_x, width), '...  18.2 us
    all_to_all x1, waiting for transfers between devices, local(): lax.all_to_all(grouped, 'sy', split_axis=1, concat_axis=1, tiled=True)  14.2 us
    all_to_all x1, waiting for transfers between devices, local(): lax.all_to_all(current.reshape(2, count_y, rows_dev // count_y, width), '...  12 us
    all_to_all x1, starting transfers between devices, local(): lax.all_to_all(current.reshape(2, count_x, rows_dev // count_x, width), '...  7.31 us
    dot_general x10, matrix products, combine(): jnp.dot(joined, matrix, preferred_element_type=jnp.float32)  7.1 us
    unnamed x59, local copies, waits for them, and re-layouts  5.51 us
  transfers between devices with their start and end apart: 3, of which 3 were waited for; matrix products, arithmetic and copies ran while one was open for 6% of the time, Pallas kernels for 0%

profile of v1, /device:TPU:0, one launch (start us, length us, event | category | flops | bytes accessed | tf_op | source)
XLA Modules:
  0.0 157.4 jit_solution(16221818404963816740)
XLA Ops:
  0.0 2.3 %copy.47 = bf16[2,8,128,256]{3,2,0,1:T(8,128)(2,1)} copy(bf16[2,8,128,256]{3,2,1,0:T(8,128)(2,1)} %bitcast.212) | data formatting | bytes 2097152 | tf_op jit(solution)/shard_map/reshape;squeeze | solution.py:77
  2.3 7.3 %all-to-all-start = ((bf16[2,8,128,256]{3,2,0,1:T(8,128)(2,1)}), bf16[2,8,128,256]{3,2,0,1:T(8,128)(2,1)S(1)}, u32[]{:S(2)}, u32[]{:S(2)}) async-start(bf16[2,8,128,256]{3,2,0,1:T(8,128)(2,1)} %copy.47), calls=%async_computation | async-start | bytes 2097152 | tf_op jit(solution)/shard_map/all_to_all | solution.py:76
  9.6 1.9 %slice_bitcast_fusion = (bf16[2,2,256,256]{3,2,1,0:T(8,128)(2,1)S(1)}, bf16[2,2,256,256]{3,2,1,0:T(8,128)(2,1)S(1)}, bf16[2,2,256,256]{3,2,1,0:T(8,128)(2,1)S(1)...) fusion(bf16[5,2,2,256,256]{4,3,2,1,0:T(8,128)(2,1)} %param.5), kind=kLoop, calls=%fused_computation.162 | loop fusion | bytes 5242880 | tf_op jit(solution)/shard_map/squeeze | solution.py:96
  11.5 0.7 slice_bitcast_fusion.23
  12.2 0.7 fusion.156
  13.0 0.9 maximum_multiply_fusion
  13.9 0.8 slice_bitcast_fusion.15
  14.7 0.9 maximum_multiply_fusion.2
  15.6 0.8 fusion.160
  16.3 0.9 maximum_multiply_fusion.4
  17.2 18.2 %all-to-all-done = bf16[2,8,128,256]{3,2,0,1:T(8,128)(2,1)S(1)} async-done(((bf16[2,8,128,256]{3,2,0,1:T(8,128)(2,1)}), bf16[2,8,128,256]{3,2,0,1:T(8,128)(2,1)S(1)}, u32[]{:S(2)}, u32[]{:S(2)}) %all-to-all-start) | async-done | bytes 1048608 | tf_op jit(solution)/shard_map/all_to_all | solution.py:76
  35.5 0.8 copy-done.23
  36.4 0.7 convolution_convert_fusion.9
  37.5 0.7 convolution_convert_fusion.8
  39.4 0.7 convolution_convert_fusion.7
  40.4 0.7 convolution_convert_fusion.6
  42.3 0.7 convolution_convert_fusion.5
  43.4 0.7 convolution_convert_fusion.4
  44.5 29.3 %all_to_all.20 = bf16[2,8,128,256]{3,2,0,1:T(8,128)(2,1)S(1)} all-to-all(bf16[2,8,128,256]{3,2,0,1:T(8,128)(2,1)S(1)} %copy.56), channel_id=1, replica_groups=mesh['sx'=8,'sy'=4] {'sx'}, dimensions={1} | all-to-all | bytes 2097152 | tf_op jit(solution)/shard_map/all_to_all | solution.py:85
  73.9 1.1 copy.58
  75.0 3.5 %all-to-all-start.2 = ((bf16[2,4,256,256]{3,2,0,1:T(8,128)(2,1)}), bf16[2,4,256,256]{3,2,0,1:T(8,128)(2,1)S(1)}, u32[]{:S(2)}, u32[]{:S(2)}) async-start(bf16[2,4,256,256]{3,2,0,1:T(8,128)(2,1)} %copy.58), calls=%async_computation.2 | async-start | bytes 2097152 | tf_op jit(solution)/shard_map/all_to_all | solution.py:88
  78.5 0.8 slice_bitcast_fusion.7
  79.3 0.9 maximum_multiply_fusion.6
  80.9 12.0 %all-to-all-done.2 = bf16[2,4,256,256]{3,2,0,1:T(8,128)(2,1)S(1)} async-done(((bf16[2,4,256,256]{3,2,0,1:T(8,128)(2,1)}), bf16[2,4,256,256]{3,2,0,1:T(8,128)(2,1)S(1)}, u32[]{:S(2)}, u32[]{:S(2)}) %all-to-all-start.2) | async-done | bytes 1048608 | tf_op jit(solution)/shard_map/all_to_all | solution.py:88
  93.0 0.7 convolution_convert_fusion.3
  94.1 0.7 convolution_convert_fusion.2
  96.0 0.7 convolution_convert_fusion.1
  96.7 0.7 convolution_convert_fusion
  97.8 1.1 copy.65
  98.9 3.5 %all-to-all-start.3 = ((bf16[2,4,256,256]{3,2,0,1:T(8,128)(2,1)}), bf16[2,4,256,256]{3,2,0,1:T(8,128)(2,1)S(1)}, u32[]{:S(2)}, u32[]{:S(2)}) async-start(bf16[2,4,256,256]{3,2,0,1:T(8,128)(2,1)} %copy.65), calls=%async_computation.3 | async-start | bytes 2097152 | tf_op jit(solution)/shard_map/all_to_all | solution.py:97
  102.6 14.2 %all-to-all-done.3 = bf16[2,4,256,256]{3,2,0,1:T(8,128)(2,1)S(1)} async-done(((bf16[2,4,256,256]{3,2,0,1:T(8,128)(2,1)}), bf16[2,4,256,256]{3,2,0,1:T(8,128)(2,1)S(1)}, u32[]{:S(2)}, u32[]{:S(2)}) %all-to-all-start.3) | async-done | bytes 1048608 | tf_op jit(solution)/shard_map/all_to_all | solution.py:97
  118.3 38.6 %all-gather.1 = f32[32,2,128]{2,1,0:T(2,128)S(1)} all-gather(f32[1,2,128]{2,1,0:T(2,128)S(1)} %maximum_bitcast_fusion.9), channel_id=2, replica_groups=mesh['sx'=8,'sy'=4] {'sx','sy'}, dimensions={0}, use_global_device_ids=true | all-gather | bytes 33792 | tf_op jit(solution)/shard_map/all_gather | solution.py:9
  (97 shorter events, 8.7 us)
Async XLA Ops:
  2.3 33.1 %all-to-all-start = ((bf16[2,8,128,256]{3,2,0,1:T(8,128)(2,1)}), bf16[2,8,128,256]{3,2,0,1:T(8,128)(2,1)S(1)}, u32[]{:S(2)}, u32[]{:S(2)}) async-start(bf16[2,8,128,256]{3,2,0,1:T(8,128)(2,1)} %copy.47), calls=%async_computation | async-start | bytes 2097152 | tf_op jit(solution)/shard_map/all_to_all | solution.py:76
  35.4 0.9 copy-start.23
  35.4 1.0 copy-start.24
  35.4 1.0 copy-start.25
  36.4 0.9 copy-start.5
  36.4 1.0 copy-start.6
  38.4 0.9 copy-start.11
  38.4 1.0 copy-start.12
  38.4 1.0 copy-start.22
  39.4 0.9 copy-start.3
  39.4 1.0 copy-start.4
  41.4 0.9 copy-start.10
  41.4 1.0 copy-start.21
  42.3 0.9 copy-start.1
  42.3 1.0 copy-start.2
  75.0 17.9 %all-to-all-start.2 = ((bf16[2,4,256,256]{3,2,0,1:T(8,128)(2,1)}), bf16[2,4,256,256]{3,2,0,1:T(8,128)(2,1)S(1)}, u32[]{:S(2)}, u32[]{:S(2)}) async-start(bf16[2,4,256,256]{3,2,0,1:T(8,128)(2,1)} %copy.58), calls=%async_computation.2 | async-start | bytes 2097152 | tf_op jit(solution)/shard_map/all_to_all | solution.py:88
  79.2 13.7 %copy-start.14 = (bf16[256,256]{1,0:T(8,128)(2,1)S(1)}, bf16[256,256]{1,0:T(8,128)(2,1)}, u32[]{:S(2)}) copy-start(bf16[256,256]{1,0:T(8,128)(2,1)} %get-tuple-element.96) | copy-start | bytes 393220
  79.2 13.7 %copy-start.16 = (bf16[256,256]{1,0:T(8,128)(2,1)S(1)}, bf16[256,256]{1,0:T(8,128)(2,1)}, u32[]{:S(2)}) copy-start(bf16[256,256]{1,0:T(8,128)(2,1)} %get-tuple-element.99) | copy-start | bytes 393220
  79.2 13.7 %copy-start.19 = (bf16[256,256]{1,0:T(8,128)(2,1)S(1)}, bf16[256,256]{1,0:T(8,128)(2,1)}, u32[]{:S(2)}) copy-start(bf16[256,256]{1,0:T(8,128)(2,1)} %get-tuple-element.107) | copy-start | bytes 393220
  93.0 1.0 copy-start.7
  93.0 1.0 copy-start.8
  93.0 1.0 copy-start.15
  93.0 1.1 copy-start.17
  93.0 1.1 copy-start.20
  95.0 0.9 copy-start.13
  95.1 1.0 copy-start.18
  97.8 4.6 %copy-start.9 = (f32[2,128,256]{2,1,0:T(8,128)S(1)}, f32[2,128,256]{2,1,0:T(8,128)}, u32[]{:S(2)}) copy-start(f32[2,128,256]{2,1,0:T(8,128)} %param.7) | copy-start | bytes 786436
  98.9 17.9 %all-to-all-start.3 = ((bf16[2,4,256,256]{3,2,0,1:T(8,128)(2,1)}), bf16[2,4,256,256]{3,2,0,1:T(8,128)(2,1)S(1)}, u32[]{:S(2)}, u32[]{:S(2)}) async-start(bf16[2,4,256,256]{3,2,0,1:T(8,128)(2,1)} %copy.65), calls=%async_computation.3 | async-start | bytes 2097152 | tf_op jit(solution)/shard_map/all_to_all | solution.py:97
  102.4 14.5 %copy-start = (bf16[2,128,1024]{2,1,0:T(8,128)(2,1)S(1)}, bf16[2,128,1024]{2,1,0:T(8,128)(2,1)}, u32[]{:S(2)}) copy-start(bf16[2,128,1024]{2,1,0:T(8,128)(2,1)} %param.6) | copy-start | bytes 1572868
